TPU v7x, 8 devices: a whole 2x2x1 slice. The times are simulated.
8 devices in a mesh: dp: 1 (over z), ep: 8 (over y, x, core).
Axes of the slice: x: 2, y: 2, z: 1, core: 2. Of those that a mesh axis runs over, the one named last changes fastest.
Arguments:
- hidden: bfloat16 [2048, 1536], P(('dp', 'ep'))
- router_w: float32 [1536, 32], replicated
- expert_ids: int32 [2048, 2], P(('dp', 'ep'))
- w_gate: bfloat16 [32, 1536, 2304], P('ep')
- w_up: bfloat16 [32, 1536, 2304], P('ep')
- w_down: bfloat16 [32, 2304, 1536], P('ep')
- post_scale: float32 [2], replicated
Outputs:
- output: bfloat16 [2048, 1536], P(('dp', 'ep'))
All inputs are finite; a program needn't handle non-finite values.
Results may differ from a plain program's by a relative error of at most 0.001.
Values are sent between devices in bfloat16 or wider.
A program may use at most 1 GiB of HBM per device.

v0:
```python
import functools

import jax
import jax.numpy as jnp
from jax import lax
from jax.experimental import pallas as pl
from jax.experimental.pallas import tpu as pltpu
from jax.sharding import PartitionSpec as P

MESH = pl.DeviceIdType.MESH
F32, BF16, I32 = jnp.float32, jnp.bfloat16, jnp.int32
NT = (((1,), (1,)), ((), ()))


def flip(idx, mask):
    out = idx
    for bit in (1, 2, 4):
        if mask & bit:
            out = out + bit - 2 * bit * ((idx // bit) % 2)
    return out


def dev(idx):
    return (lax.axis_index('dp'), idx)


def iota(shape, dim):
    return lax.broadcasted_iota(I32, shape, dim)


def weight_copies(w1, w3, w2, w1b, w3b, w2b, sem, e, f, n):
    ft = w1b.shape[2]
    cols = pl.ds(pl.multiple_of(f * ft, ft), ft)
    return (
        pltpu.make_async_copy(w1.at[e, :, cols], w1b.at[n], sem.at[n, 0]),
        pltpu.make_async_copy(w3.at[e, :, cols], w3b.at[n], sem.at[n, 1]),
        pltpu.make_async_copy(w2.at[e, cols, :], w2b.at[n], sem.at[n, 2]),
    )


def ffn_part(x, w1b, w3b, w2b, n, mid, yacc, fresh, m):
    for c in range(0, w1b.shape[2], 256):
        gate = jnp.dot(x, w1b[n, :, c:c + 256], preferred_element_type=F32)
        up = jnp.dot(x, w3b[n, :, c:c + 256], preferred_element_type=F32)
        mid[0:m, c:c + 256] = (gate * jax.nn.sigmoid(gate) * up).astype(BF16)
    for c in range(0, w2b.shape[2], 512):
        part = jnp.dot(mid[0:m, :], w2b[n, :, c:c + 512], preferred_element_type=F32)
        yacc[0:m, c:c + 512] = jnp.where(fresh, 0.0, yacc[0:m, c:c + 512]) + part


CHUNKS = 4
NF = 3
RING = 4
LATE_RING = 2
BRANCH_LANE = 127
LATE = 2


def gather_kernel(caps, hid_in, ids_in, wrt_in, scale_in, w1, w3, w2, near, far, y_own, tok, goal, plan, which, w1p, w3p, w2p, hid, ids, wrt, scale, pos, mid, yacc, land, ids_all, send, recv, id_send, id_recv, wsem, in_sem):
    me = lax.axis_index('ep')
    own = [pltpu.make_async_copy(src, dst, in_sem.at[n]) for n, (src, dst) in enumerate(((hid_in, hid), (ids_in, ids), (wrt_in, wrt), (scale_in, scale)))]
    for c in own:
        c.start()
    local, _, slots, _ = near.shape
    owners = 2 + far.shape[1]
    steps = (local - LATE) * NF

    def weights(t):
        return weight_copies(w1, w3, w2, w1p, w3p, w2p, wsem, local - 1 - t // NF, t % NF, t % RING)

    tokens, width = hid.shape
    experts = wrt.shape[0]
    rows = tokens // CHUNKS
    barrier = pltpu.get_barrier_semaphore()
    for q in range(1, owners):
        pl.semaphore_signal(barrier, inc=1, device_id=dev(flip(me, q)), device_id_type=MESH)
    pl.semaphore_wait(barrier, owners - 1)
    own[0].wait()
    own[1].wait()

    def piece(q, c):
        return (hid if q == 0 else land.at[q]).at[pl.ds(c * rows, rows)]

    def remote(q, c, n, to):
        return pltpu.make_async_remote_copy(src_ref=piece(q, c), dst_ref=land.at[q ^ to, pl.ds(c * rows, rows)], send_sem=send.at[n], recv_sem=recv.at[n], device_id=dev(flip(me, to)), device_id_type=MESH)

    id_copies = []
    for q in range(1, owners):
        id_copies.append(pltpu.make_async_remote_copy(src_ref=ids, dst_ref=ids_all.at[q], send_sem=id_send.at[q], recv_sem=id_recv.at[q], device_id=dev(flip(me, q)), device_id_type=MESH))
    x_order, y_order = (0, 1, 2, 3), (2, 3, 0, 1)
    to_x = {c: remote(0, c, c, 2) for c in x_order}
    to_y = {c: remote(0, c, 4 + c, 4) for c in y_order}
    for cx, cy in zip(x_order, y_order):
        to_x[cx].start()
        to_y[cy].start()
        if cx == 0:
            for c in id_copies:
                c.start()
    to_mate = pltpu.make_async_remote_copy(src_ref=hid, dst_ref=land.at[1], send_sem=send.at[24], recv_sem=recv.at[24], device_id=dev(flip(me, 1)), device_id_type=MESH)
    to_mate.start()
    for t in range(RING):
        for c in weights(t):
            c.start()

    own[2].wait()
    own[3].wait()
    h = hid[...]
    w = wrt[...]
    w_hi = w.astype(BF16)
    rest = w - w_hi.astype(F32)
    w_mid = rest.astype(BF16)
    w_lo = (rest - w_mid.astype(F32)).astype(BF16)
    dot = functools.partial(lax.dot_general, dimension_numbers=NT, preferred_element_type=F32)
    logits = dot(h, w_hi) + (dot(h, w_mid) + dot(h, w_lo))
    ex = jnp.exp(logits - jnp.max(logits, axis=1, keepdims=True))
    prob = ex / jnp.sum(ex, axis=1, keepdims=True)
    ta, tb = iota((tokens, tokens), 0), iota((tokens, tokens), 1)
    eye = (ta == tb).astype(F32).astype(BF16)
    own_ids = ids[...].astype(F32)
    lane = iota((tokens, experts), 1).astype(F32)
    id_col = [dot(eye, jnp.broadcast_to(own_ids[k:k + 1], (8, tokens)).astype(BF16))[:, 0:1] for k in (0, 1)]
    pick = [(id_col[k] == lane).astype(F32) for k in (0, 1)]
    g = [jnp.sum(pick[k] * prob, axis=1, keepdims=True) for k in (0, 1)]
    total = g[0] + g[1]

    for c in id_copies:
        c.wait_recv()
    ids_all[0] = ids[...]
    counts = []
    for q in range(owners):
        both = ids_all[q]
        e_col = iota((experts, tokens), 0)
        hot = ((both[0:1] == e_col) | (both[1:2] == e_col)).astype(F32).astype(BF16)
        counts.append(dot(jnp.ones((8, tokens), BF16), hot))
    most = functools.reduce(jnp.maximum, counts)
    count = jnp.concatenate([c[0:1] for c in counts], axis=0)
    stride = jnp.where(most > 32.0, float(slots), jnp.where(most > 16.0, 32.0, 16.0))
    mark = lambda mask: mask.astype(F32).astype(BF16)
    plain = functools.partial(jnp.dot, preferred_element_type=F32)
    ea, eb = iota((experts, experts), 0), iota((experts, experts), 1)
    same, same_chip = ea // local == eb // local, ea // (2 * local) == eb // (2 * local)
    offset = plain(stride.astype(BF16), mark(same & (ea < eb)))
    need = jnp.max(plain(stride.astype(BF16), mark(same)), axis=1, keepdims=True)[0:1]
    need_chip = jnp.max(jnp.max(plain(count.astype(BF16), mark(same_chip)), axis=1, keepdims=True), axis=0, keepdims=True)
    branch = jnp.zeros((1, 1), F32)
    for limit, limit_chip in caps[:-1]:
        branch = branch + ((need > limit) | (need_chip > limit_chip)).astype(F32)
    which[0] = jnp.max(branch).astype(I32)
    rank = plain(mark(tb < ta), (pick[0] + pick[1]).astype(BF16))
    chip_first = plain(count.astype(BF16), mark(same_chip & (ea < eb)))[0:1]
    local_of = lane - jnp.floor(lane * (1.0 / local)) * local
    late_place = jnp.where(local_of < LATE, local_of * slots + rank, -1.0)
    late = [jnp.sum(pick[k] * late_place, axis=1, keepdims=True) for k in (0, 1)]
    slot = [jnp.sum(pick[k] * (rank + offset[0:1]), axis=1, keepdims=True) for k in (0, 1)]
    packed = [jnp.sum(pick[k] * (rank + chip_first), axis=1, keepdims=True) for k in (0, 1)]
    owner = [jnp.floor(id_col[k] * (1.0 / local)) for k in (0, 1)]
    wide = iota((tokens, 128), 1)
    table = jnp.zeros((tokens, 128), F32)
    for n, col in enumerate((g[0] / total, g[1] / total, *owner, *slot, *packed, *late, scale[0], scale[1])):
        table = jnp.where(wide == n, col, table)
    tok[...] = table

    e_row, n_col = iota((experts, 128), 0), iota((experts, 128), 1)
    e_of = jnp.where(n_col < local, me * local + n_col, flip(me, 1) * local + n_col - local)
    used = n_col < 2 * local
    held = plain(count.astype(BF16), mark(used & (e_row == e_of)))
    start = plain(count.astype(BF16), mark(used & (e_row // (2 * local) == me // 2) & (e_row < e_of)))
    base = plain(stride.astype(BF16), mark(used & (e_row // local == e_of // local) & (e_row < e_of)))
    base_size = plain(stride.astype(BF16), mark(used & (e_row == e_of)))
    lane_of = iota((owners, goal.shape[1]), 1)
    where_to = jnp.full((owners, goal.shape[1]), -1.0, F32)
    for n in range(2 * local):
        at = (lane_of - (n // local) * (goal.shape[1] // 2)).astype(F32) - base[0:1, n:n + 1]
        where_to = jnp.where((at >= 0.0) & (at < held[:, n:n + 1]), at + start[:, n:n + 1], where_to)
    goal[...] = where_to

    first, second = (jnp.concatenate([ids_all[q, k:k + 1] for q in range(owners)], axis=0) for k in (0, 1))
    marks = jnp.concatenate([((first == me * local + j) | (second == me * local + j)).astype(F32) for j in range(local)], axis=0)
    earlier = plain(marks.astype(BF16), (ta < tb).astype(F32).astype(BF16))
    pos[...] = jnp.where(marks > 0.5, earlier, -1.0)
    plan[...] = jnp.where(n_col[0:8] == BRANCH_LANE, branch, base_size).astype(I32)

    def pick_rows(q):
        at = iota((slots, tokens), 0).astype(F32)
        match = jnp.concatenate([(at == pos[j * owners + q:j * owners + q + 1, :]).astype(F32) for j in range(local)], axis=0).astype(BF16)

        def columns(cols):
            block = hid[:, cols] if q == 0 else land[q, :, cols]
            part = jnp.dot(match, block, preferred_element_type=F32).astype(BF16)
            for j in range(local):
                to = near.at[j, q] if q < 2 else far.at[j, q - 2]
                to[:, cols] = part[j * slots:(j + 1) * slots]

        if q < 6:
            @pl.loop(0, width // 512)
            def _(n):
                columns(pl.ds(pl.multiple_of(n * 512, 512), 512))
        else:
            for c in range(0, width, 512):
                columns(pl.ds(c, 512))

    def own_steps(first, last):
        @pl.loop(first, last)
        def _(t):
            e, f, n = local - 1 - t // NF, t % NF, t % RING
            for c in weights(t):
                c.wait()
            x = near[e, :, :, :].reshape(2 * slots, width)
            ffn_part(x, w1p, w3p, w2p, n, mid, yacc, f == 0, 2 * slots)

            @pl.when(f == NF - 1)
            def _():
                for q in (0, 1):
                    y_own[e - LATE, q, :, :] = yacc[q * slots:(q + 1) * slots, :].astype(BF16)

            @pl.when(t + RING < steps)
            def _():
                for c in weights(t + RING):
                    c.start()

    sent = [*to_x.values(), *to_y.values(), to_mate]

    def pass_on(q, c, n, to):
        copy = remote(q, c, n, to)
        copy.start()
        sent.append(copy)
        return copy

    pick_rows(0)
    to_mate.wait_recv()
    pick_rows(1)
    across, mates = {}, {2: [], 4: [], 6: []}
    for n, (cx, cy) in enumerate(zip(x_order, y_order)):
        if n < 2:
            own_steps(n * steps // 2, (n + 1) * steps // 2)
        to_x[cx].wait_recv()
        if cx in (0, 1):
            across[cx] = pass_on(2, cx, 8 + cx, 4)
        mates[2].append(pass_on(2, cx, 12 + cx, 1))
        to_y[cy].wait_recv()
        if cy in (2, 3):
            across[cy] = pass_on(4, cy, 8 + cy, 2)
        mates[4].append(pass_on(4, cy, 16 + cy, 1))
    for q in (2, 4):
        pick_rows(q)
    for q in (2, 4):
        for m in mates[q]:
            m.wait_recv()
        pick_rows(q + 1)
    for c in (0, 2, 1, 3):
        across[c].wait_recv()
        mates[6].append(pass_on(6, c, 20 + c, 1))
    pick_rows(6)
    for m in mates[6]:
        m.wait_recv()
    pick_rows(7)
    for m in sent:
        m.wait_send()
    for c in id_copies:
        c.wait_send()


def gather_call(hidden, ids_t, wr_t, scale, w1, w3, w2, owners, caps):
    tokens, width = hidden.shape
    experts = wr_t.shape[0]
    local, _, ffn = w1.shape
    slots = caps[-1][0] // local
    ft = ffn // NF
    vmem = pl.BlockSpec(memory_space=pltpu.VMEM)
    hbm = pl.BlockSpec(memory_space=pl.ANY)
    return pl.pallas_call(
        functools.partial(gather_kernel, caps),
        name='gather_tokens',
        out_shape=(
            pltpu.VMEM((local, 2, slots, width), BF16),
            pltpu.VMEM((local, owners - 2, slots, width), BF16),
            pltpu.VMEM((local - LATE, 2, slots, width), BF16),
            jax.ShapeDtypeStruct((tokens, 128), F32),
            jax.ShapeDtypeStruct((owners, 2 * local * slots), F32),
            jax.ShapeDtypeStruct((8, 128), I32),
            jax.ShapeDtypeStruct((1,), I32),
            pltpu.VMEM((RING, width, ft), BF16),
            pltpu.VMEM((RING, width, ft), BF16),
            pltpu.VMEM((RING, ft, width), BF16),
        ),
        in_specs=[hbm, *[pl.BlockSpec(memory_space=pltpu.HBM)] * 3, hbm, hbm, hbm],
        out_specs=(*[vmem] * 6, pl.BlockSpec(memory_space=pltpu.SMEM), *[vmem] * 3),
        scratch_shapes=[
            pltpu.VMEM((tokens, width), BF16),
            pltpu.VMEM((2, tokens), I32),
            pltpu.VMEM((experts, width), F32),
            pltpu.SMEM((2,), F32),
            pltpu.VMEM((local * owners, tokens), F32),
            pltpu.VMEM((2 * slots, ft), BF16),
            pltpu.VMEM((2 * slots, width), F32),
            pltpu.VMEM((owners, tokens, width), BF16),
            pltpu.VMEM((owners, 2, tokens), I32),
            pltpu.SemaphoreType.DMA((25,)),
            pltpu.SemaphoreType.DMA((25,)),
            pltpu.SemaphoreType.DMA((owners,)),
            pltpu.SemaphoreType.DMA((owners,)),
            pltpu.SemaphoreType.DMA((RING, 3)),
            pltpu.SemaphoreType.DMA((4,)),
        ],
        compiler_params=pltpu.CompilerParams(collective_id=0, has_side_effects=True, vmem_limit_bytes=13 * 1024 * 1024),
    )(hidden, *(pltpu.with_memory_space_constraint(x, pltpu.HBM) for x in (ids_t, wr_t, scale)), w1, w3, w2)


def expert_kernel(caps, info, rows, y_own, _w1b, _w3b, _w2b, w1, w3, w2, ret, w1b, w3b, w2b, mid, yacc, plan, wsem):
    local, distant, slots, width = rows.shape
    owners = distant + 2
    steps = local * NF
    done = (local - LATE) * NF

    size = [info[0, j] for j in range(local)]
    branch = info[0, BRANCH_LANE]
    for j in range(local):
        rank = jnp.int32(j - LATE if j >= LATE else local - LATE)
        offset = jnp.int32(0)
        for i in range(local):
            if i < LATE and j < LATE and i != j:
                ahead = (size[i] >= size[j]) if i < j else (size[i] > size[j])
                rank = rank + ahead.astype(I32)
            if i < j:
                offset = offset + size[i]
        plan[0, rank] = jnp.int32(j)
        plan[1, rank] = size[j]
        plan[2, rank] = offset
    used = size[0]
    for j in range(1, local):
        used = used + size[j]

    def part_of(t):
        turn = jnp.where(t < NF, 0, 2 * NF - RING)
        return (t % NF + turn) % NF

    def weights(t):
        return weight_copies(w1, w3, w2, w1b, w3b, w2b, wsem, plan[0, t // NF], part_of(t), (t + done - NF) % RING)

    limit = jnp.int32(caps[0][0])
    for n in range(1, len(caps)):
        limit = jnp.where(branch >= n, caps[n][0], limit)

    @pl.loop(used // 16, limit // 16)
    def _(n):
        blank = pl.ds(pl.multiple_of(n * 16, 16), 16)
        for q in range(owners):
            ret[q, blank, :] = jnp.zeros((16, width), BF16)

    @pl.loop(0, steps)
    def _(t):
        r, f, n = t // NF, t % NF, (t + done - NF) % RING
        e = plan[0, r]

        @pl.when(t >= RING)
        def _():
            for c in weights(t):
                c.wait()

        for size in (16, 32, slots):
            m = size * distant

            @pl.when(plan[1, r] == size)
            def _():
                x = rows[e, :, 0:size, :].reshape(m, width)
                ffn_part(x, w1b, w3b, w2b, n, mid, yacc, f == 0, m)

                @pl.when(f == NF - 1)
                def _():
                    first = pl.multiple_of(plan[2, r], 16)
                    for q in (0, 1):
                        mine = y_own[jnp.maximum(e - LATE, 0), q, 0:size, :]
                        ret[q, pl.ds(first, size), :] = jnp.where(e >= LATE, mine, jnp.zeros_like(mine))
                    for q in range(2, owners):
                        ret[q, pl.ds(first, size), :] = yacc[(q - 2) * size:(q - 1) * size, :].astype(BF16)

        @pl.when(t + RING < steps)
        def _():
            for c in weights(t + RING):
                c.start()


def expert_call(sizes, rows, y_own, w1p, w3p, w2p, w1, w3, w2, caps):
    local, distant, slots, width = rows.shape
    owners = distant + 2
    ft = w1p.shape[2]
    hbm = pl.BlockSpec(memory_space=pl.ANY)
    vmem = pl.BlockSpec(memory_space=pltpu.VMEM)
    flops = 3 * 2 * local * slots * owners * width * ft * NF // 2
    return pl.pallas_call(
        functools.partial(expert_kernel, caps),
        name='experts',
        out_shape=(
            pltpu.VMEM((owners, caps[-1][0], width), BF16),
            pltpu.VMEM(w1p.shape, BF16),
            pltpu.VMEM(w3p.shape, BF16),
            pltpu.VMEM(w2p.shape, BF16),
        ),
        in_specs=[vmem] * 6 + [hbm] * 3,
        out_specs=(vmem, vmem, vmem, vmem),
        input_output_aliases={3: 1, 4: 2, 5: 3},
        scratch_shapes=[
            pltpu.VMEM((distant * slots, ft), BF16),
            pltpu.VMEM((distant * slots, width), F32),
            pltpu.SMEM((3, local), I32),
            pltpu.SemaphoreType.DMA((RING, 3)),
        ],
        compiler_params=pltpu.CompilerParams(vmem_limit_bytes=12 * 1024 * 1024),
        cost_estimate=pl.CostEstimate(flops=flops, bytes_accessed=3 * 2 * local * width * ft * NF, transcendentals=0),
    )(sizes, rows, y_own, w1p, w3p, w2p, w1, w3, w2)[0]


REMOTE = (2, 4, 6)


def return_kernel(cap, chip_cap, ret, near, tok, goal, hid, w1, w3, w2, out, half, pack, got, acc, late, late_half, mid, yacc, w1b, w3b, w2b, send, recv, half_send, half_recv, wsem):
    me = lax.axis_index('ep')
    slots = near.shape[2]
    steps = LATE * NF

    def weights(t):
        return weight_copies(w1, w3, w2, w1b, w3b, w2b, wsem, t // NF, t % NF, t % LATE_RING)

    tokens, width = hid.shape
    lanes = goal.shape[1] // 2
    barrier = pltpu.get_barrier_semaphore()
    for q in (1, *REMOTE):
        pl.semaphore_signal(barrier, inc=1, device_id=dev(flip(me, q)), device_id_type=MESH)
    pl.semaphore_wait(barrier, 1 + len(REMOTE))
    halves, copies = {}, {}
    for q in (*REMOTE, 0):
        halves[q] = pltpu.make_async_remote_copy(src_ref=ret.at[q + 1, pl.ds(0, cap)], dst_ref=half.at[q // 2], send_sem=half_send.at[q // 2], recv_sem=half_recv.at[q // 2], device_id=dev(flip(me, 1)), device_id_type=MESH)
        halves[q].start()

    for q in REMOTE:
        row = iota((chip_cap, cap), 0).astype(F32)
        mine = (row == goal[q:q + 1, 0:cap]).astype(F32).astype(BF16)
        theirs = (row == goal[q:q + 1, lanes:lanes + cap]).astype(F32).astype(BF16)
        halves[q].wait_recv()
        for c in range(0, width, 512):
            part = jnp.dot(mine, ret[q, 0:cap, c:c + 512], preferred_element_type=F32)
            part = part + jnp.dot(theirs, half[q // 2, :, c:c + 512], preferred_element_type=F32)
            pack[q // 2 - 1, :, c:c + 512] = part.astype(BF16)
        copies[q] = pltpu.make_async_remote_copy(src_ref=pack.at[q // 2 - 1], dst_ref=got.at[q // 2 - 1], send_sem=send.at[q // 2 - 1], recv_sem=recv.at[q // 2 - 1], device_id=dev(flip(me, q)), device_id_type=MESH)
        copies[q].start()

    for t in range(LATE_RING):
        for c in weights(t):
            c.start()
    table = tok[...]

    def chosen(column, peer, at, count):
        lane = iota((tokens, count), 1).astype(F32)
        return jnp.concatenate([((column[k] == peer) & (table[:, at + k:at + k + 1] == lane)).astype(F32) for k in (0, 1)], axis=0).astype(BF16)

    owner = [table[:, 2 + k:3 + k] for k in (0, 1)]
    chip = [jnp.floor(o * 0.5) for o in owner]

    gate = [table[:, k:k + 1] for k in (0, 1)]
    scale = [table[:, 10 + k:11 + k] for k in (0, 1)]

    def add(pick, block, fresh=False, last=False):
        @pl.loop(0, width // 512)
        def _(n):
            cols = pl.ds(pl.multiple_of(n * 512, 512), 512)
            part = jnp.dot(pick, block(cols), preferred_element_type=F32)
            mixed = gate[0] * part[0:tokens] + gate[1] * part[tokens:2 * tokens]
            if not fresh:
                mixed = acc[:, cols] + mixed
            if last:
                out[:, cols] = (scale[0] * hid[:, cols].astype(F32) + scale[1] * mixed).astype(BF16)
            else:
                acc[:, cols] = mixed

    add(chosen(owner, me.astype(F32), 4, cap), lambda c: ret[0, 0:cap, c], fresh=True)
    pick = chosen(owner, flip(me, 1).astype(F32), 4, cap)
    halves[0].wait_recv()
    add(pick, lambda c: half[0, :, c])

    @pl.loop(0, steps)
    def _(t):
        e, f, n = t // NF, t % NF, t % LATE_RING
        for c in weights(t):
            c.wait()
        ffn_part(near[e, :, :, :].reshape(2 * slots, width), w1b, w3b, w2b, n, mid, yacc, f == 0, 2 * slots)

        @pl.when(f == NF - 1)
        def _():
            for q in (0, 1):
                late[q, pl.ds(pl.multiple_of(e * slots, slots), slots), :] = yacc[q * slots:(q + 1) * slots, :].astype(BF16)

        @pl.when(t + LATE_RING < steps)
        def _():
            for c in weights(t + LATE_RING):
                c.start()

    swap = pltpu.make_async_remote_copy(src_ref=late.at[1], dst_ref=late_half, send_sem=half_send.at[4], recv_sem=half_recv.at[4], device_id=dev(flip(me, 1)), device_id_type=MESH)
    swap.start()
    add(chosen(owner, me.astype(F32), 8, LATE * slots), lambda c: late[0, :, c])
    pick = chosen(owner, flip(me, 1).astype(F32), 8, LATE * slots)
    swap.wait_recv()
    add(pick, lambda c: late_half[:, c])
    for q in REMOTE:
        pick = chosen(chip, (flip(me, q) // 2).astype(F32), 6, chip_cap)
        copies[q].wait_recv()
        add(pick, lambda c: got[q // 2 - 1, :, c], last=q == REMOTE[-1])

    for copy in (*halves.values(), *copies.values(), swap):
        copy.wait_send()


def return_call(n, caps, ret, near, tok, goal, hidden, w1, w3, w2):
    owners, _, width = ret.shape
    slots, ft = near.shape[2], w1.shape[2] // NF
    tokens = hidden.shape[0]
    cap, chip_cap = caps
    vmem = pl.BlockSpec(memory_space=pltpu.VMEM)
    return pl.pallas_call(
        functools.partial(return_kernel, cap, chip_cap),
        name=f'return_{cap}_{chip_cap}',
        out_shape=jax.ShapeDtypeStruct((tokens, width), BF16),
        in_specs=[vmem] * 5 + [pl.BlockSpec(memory_space=pl.ANY)] * 3,
        out_specs=vmem,
        scratch_shapes=[
            pltpu.VMEM((owners // 2, cap, width), BF16),
            pltpu.VMEM((len(REMOTE), chip_cap, width), BF16),
            pltpu.VMEM((len(REMOTE), chip_cap, width), BF16),
            pltpu.VMEM((tokens, width), F32),
            pltpu.VMEM((2, LATE * slots, width), BF16),
            pltpu.VMEM((LATE * slots, width), BF16),
            pltpu.VMEM((2 * slots, ft), BF16),
            pltpu.VMEM((2 * slots, width), F32),
            pltpu.VMEM((LATE_RING, width, ft), BF16),
            pltpu.VMEM((LATE_RING, width, ft), BF16),
            pltpu.VMEM((LATE_RING, ft, width), BF16),
            pltpu.SemaphoreType.DMA((len(REMOTE),)),
            pltpu.SemaphoreType.DMA((len(REMOTE),)),
            pltpu.SemaphoreType.DMA((owners // 2 + 1,)),
            pltpu.SemaphoreType.DMA((owners // 2 + 1,)),
            pltpu.SemaphoreType.DMA((LATE_RING, 3)),
        ],
        compiler_params=pltpu.CompilerParams(collective_id=1 + n, has_side_effects=True, vmem_limit_bytes=34 * 1024 * 1024),
    )(ret, near, tok, goal, hidden, w1, w3, w2)


def capacities(local, slots):
    full = [slots * n + 16 * (local - n) for n in range(1, local + 1)]
    chip = [2 * slots + 8 + (slots - 8) * n for n in range(local - 1)]
    return (*zip(full, chip), (local * slots, 2 * local * slots))


def solution(mesh):
    owners = mesh.shape['ep']

    def local_step(hidden, router_w, expert_ids, w_gate, w_up, w_down, post_scale):
        tokens = hidden.shape[0]
        local = w_gate.shape[0]
        slots = tokens // max(1, local * owners // 8)
        caps = capacities(local, slots)
        near, far, y_own, tok, goal, plan, which, w1p, w3p, w2p = gather_call(hidden, expert_ids.T, router_w.T, post_scale, w_gate, w_up, w_down, owners, caps)
        ret = expert_call(plan, far, y_own, w1p, w3p, w2p, w_gate, w_up, w_down, caps)
        branches = [functools.partial(return_call, n, cap) for n, cap in enumerate(caps)]
        return lax.switch(which[0], branches, ret, near, tok, goal, hidden, w_gate, w_up, w_down)

    tok_spec = P(('dp', 'ep'))
    return jax.shard_map(local_step, mesh=mesh, in_specs=(tok_spec, P(), tok_spec, P('ep'), P('ep'), P('ep'), P()), out_specs=tok_spec, check_vma=False)
```

profile of v0, /device:TPU:0, one launch (start us, length us, event | category | flops | bytes accessed | tf_op | source)
XLA Modules:
  0.0 94.0 jit_solution(17660196780762896864)
XLA Ops:
  0.0 33.9 %gather_tokens.1 = (bf16[4,2,64,1536]{3,2,1,0:T(8,128)(2,1)S(1)}, bf16[4,6,64,1536]{3,2,1,0:T(8,128)(2,1)S(1)}, bf16[2,2,64,1536]{3,2,1,0:T(8,128)(2,1)S(1)}, f3...) custom-call(bf16[256,1536]{1,0:T(8,128)(2,1)} %hid_in.1, ...), custom_call_target="tpu_custom_call" | custom-call | tf_op jit(solution)/shard_map/gather_tokens/pallas_call | solution.py:271
  34.5 0.0 copy-start
  34.5 20.8 %experts.1 = (bf16[8,256,1536]{2,1,0:T(8,128)(2,1)S(1)}, bf16[4,1536,768]{2,1,0:T(8,128)(2,1)S(1)}, bf16[4,1536,768]{2,1,0:T(8,128)(2,1)S(1)}, bf16[4,768,1536]{2,1,0:T(8,128)(2,1)S(1)}) custom-call(s32[8,128]{1,0:T(8,128)S(1)} %get-tuple-element.118.info, ...), custom_call_target="tpu_custom_call", output_to_operand_aliasing={{1}: (3, {}), {2}: (4, {}), {3}: (5, {})} | custom-call | flops 21743271936 | bytes 84934656 | tf_op jit(solution)/shard_map/experts/pallas_call | solution.py:390
  55.2 0.0 copy-done
  55.2 37.9 %conditional.1 = (bf16[256,1536]{1,0:T(8,128)(2,1)S(1)}) conditional(s32[]{:T(128)} %bitcast.2, (bf16[8,256,1536]{2,1,0:T(8,128)(2,1)S(1)}, bf16[4,2,64,1536]{3,2,1,0:T(8,128)(2,1)S(1)}, f32[256,128]{1,0:T(8,128)S(1)}, f32[8,512]{1,0:T(8,128)S(1)}, bf16[256,1536]{1,0:T(8,128)(2,1)S(1)}, ...), branch_computations={%region_0.0_spmd, %region_1.0_spmd, %region_2.0_spmd, %region_3.0_... | conditional | bytes 8 | solution.py:563
  55.5 37.5 %return_160_192.1 = bf16[256,1536]{1,0:T(8,128)(2,1)S(1)} custom-call(bf16[8,256,1536]{2,1,0:T(8,128)(2,1)S(1)} %get-tuple-element.82.ret, bf16[4,2,64,1536]{3,2,1,0:T(8,128)(2,1)S(1)} %get-tuple-element.83.near, f32[256,128]{1,0:T(8,128)S(1)} %get-tuple-element.84.tok, f32[8,512]{1,0:T(8,128)S(1)} %get-tuple-element.85.goal, ...), custom_call_target="tpu_custom_call" | custom-call | tf_op jit(solution)/shard_map/cond/branch_1_fun/return_160_192/pallas_call | solution.py:518
  93.2 0.9 copy.23
Async XLA Ops:
  34.5 20.8 %copy-start = (bf16[256,1536]{1,0:T(8,128)(2,1)S(1)}, bf16[256,1536]{1,0:T(8,128)(2,1)}, u32[]{:S(2)}) copy-start(bf16[256,1536]{1,0:T(8,128)(2,1)} %hid_in.1) | copy-start | bytes 2359300
where the time goes:
time: 95 us; the launch traced here: 94 us
  Pallas kernels  92.1 us (97%)
    pallas_call x1, Pallas kernels, return_call(): pl.pallas_call(functools.partial(return_kernel, cap, chip_cap), name=f're...  37.5 us
    pallas_call x1, Pallas kernels, gather_call(): pl.pallas_call(functools.partial(gather_kernel, caps), name='gather_token...  33.9 us
    pallas_call x1, Pallas kernels, expert_call(): pl.pallas_call(functools.partial(expert_kernel, caps), name='experts', ou...  20.8 us

commit v1 on v0

--- a/solution.py
+++ b/solution.py
@@ -145,7 +145,7 @@
     branch = jnp.zeros((1, 1), F32)
     for limit, limit_chip in caps[:-1]:
         branch = branch + ((need > limit) | (need_chip > limit_chip)).astype(F32)
-    which[0] = jnp.max(branch).astype(I32)
+    which[...] = branch.astype(I32)
     rank = plain(mark(tb < ta), (pick[0] + pick[1]).astype(BF16))
     chip_first = plain(count.astype(BF16), mark(same_chip & (ea < eb)))[0:1]
     local_of = lane - jnp.floor(lane * (1.0 / local)) * local
@@ -278,13 +278,13 @@
             jax.ShapeDtypeStruct((tokens, 128), F32),
             jax.ShapeDtypeStruct((owners, 2 * local * slots), F32),
             jax.ShapeDtypeStruct((8, 128), I32),
-            jax.ShapeDtypeStruct((1,), I32),
+            jax.ShapeDtypeStruct((1, 1), I32),
             pltpu.VMEM((RING, width, ft), BF16),
             pltpu.VMEM((RING, width, ft), BF16),
             pltpu.VMEM((RING, ft, width), BF16),
         ),
         in_specs=[hbm, *[pl.BlockSpec(memory_space=pltpu.HBM)] * 3, hbm, hbm, hbm],
-        out_specs=(*[vmem] * 6, pl.BlockSpec(memory_space=pltpu.SMEM), *[vmem] * 3),
+        out_specs=(vmem,) * 10,
         scratch_shapes=[
             pltpu.VMEM((tokens, width), BF16),
             pltpu.VMEM((2, tokens), I32),
@@ -560,7 +560,7 @@
         near, far, y_own, tok, goal, plan, which, w1p, w3p, w2p = gather_call(hidden, expert_ids.T, router_w.T, post_scale, w_gate, w_up, w_down, owners, caps)
         ret = expert_call(plan, far, y_own, w1p, w3p, w2p, w_gate, w_up, w_down, caps)
         branches = [functools.partial(return_call, n, cap) for n, cap in enumerate(caps)]
-        return lax.switch(which[0], branches, ret, near, tok, goal, hidden, w_gate, w_up, w_down)
+        return lax.switch(which.reshape(()), branches, ret, near, tok, goal, hidden, w_gate, w_up, w_down)
 
     tok_spec = P(('dp', 'ep'))
     return jax.shard_map(local_step, mesh=mesh, in_specs=(tok_spec, P(), tok_spec, P('ep'), P('ep'), P('ep'), P()), out_specs=tok_spec, check_vma=False)

time: 95 us -> 94.7 us (level)
    pallas_call x1, Pallas kernels: 37.5 us -> 33 us  [return_call(): pl.pallas_call(functools.partial(return_kernel, cap, chip_cap), name=f're...]
    pallas_call x1, Pallas kernels: 20.8 us -> 24.3 us  [expert_call(): pl.pallas_call(functools.partial(expert_kernel, caps), name='experts', ou...]
where the time goes in v1:
time: 94.7 us; the launch traced here: 93.1 us
  Pallas kernels  91.2 us (96%)
    pallas_call x1, Pallas kernels, gather_call(): pl.pallas_call(functools.partial(gather_kernel, caps), name='gather_token...  33.9 us
    pallas_call x1, Pallas kernels, return_call(): pl.pallas_call(functools.partial(return_kernel, cap, chip_cap), name=f're...  33 us
    pallas_call x1, Pallas kernels, expert_call(): pl.pallas_call(functools.partial(expert_kernel, caps), name='experts', ou...  24.3 us

profile of v1, /device:TPU:0, one launch (start us, length us, event | category | flops | bytes accessed | tf_op | source)
XLA Modules:
  0.0 93.1 jit_solution(13402323902341985174)
XLA Ops:
  0.0 33.9 %gather_tokens.1 = (bf16[4,2,64,1536]{3,2,1,0:T(8,128)(2,1)S(1)}, bf16[4,6,64,1536]{3,2,1,0:T(8,128)(2,1)S(1)}, bf16[2,2,64,1536]{3,2,1,0:T(8,128)(2,1)S(1)}, f3...) custom-call(bf16[256,1536]{1,0:T(8,128)(2,1)} %hid_in.1, ...), custom_call_target="tpu_custom_call" | custom-call | tf_op jit(solution)/shard_map/gather_tokens/pallas_call | solution.py:271
  34.5 0.0 copy-start
  34.5 24.3 %experts.1 = (bf16[8,256,1536]{2,1,0:T(8,128)(2,1)S(1)}, bf16[4,1536,768]{2,1,0:T(8,128)(2,1)S(1)}, bf16[4,1536,768]{2,1,0:T(8,128)(2,1)S(1)}, bf16[4,768,1536]{2,1,0:T(8,128)(2,1)S(1)}) custom-call(s32[8,128]{1,0:T(8,128)S(1)} %get-tuple-element.118.info, ...), custom_call_target="tpu_custom_call", output_to_operand_aliasing={{1}: (3, {}), {2}: (4, {}), {3}: (5, {})} | custom-call | flops 21743271936 | bytes 84934656 | tf_op jit(solution)/shard_map/experts/pallas_call | solution.py:390
  58.8 0.0 copy-done
  58.8 33.4 %conditional.1 = (bf16[256,1536]{1,0:T(8,128)(2,1)S(1)}) conditional(s32[]{:T(128)} %bitcast.2, (bf16[8,256,1536]{2,1,0:T(8,128)(2,1)S(1)}, bf16[4,2,64,1536]{3,2,1,0:T(8,128)(2,1)S(1)}, f32[256,128]{1,0:T(8,128)S(1)}, f32[8,512]{1,0:T(8,128)S(1)}, bf16[256,1536]{1,0:T(8,128)(2,1)S(1)}, ...), branch_computations={%region_0.0_spmd, %region_1.0_spmd, %region_2.0_spmd, %region_3.0_... | conditional | bytes 8 | solution.py:563
  59.0 33.0 %return_160_192.1 = bf16[256,1536]{1,0:T(8,128)(2,1)S(1)} custom-call(bf16[8,256,1536]{2,1,0:T(8,128)(2,1)S(1)} %get-tuple-element.82.ret, bf16[4,2,64,1536]{3,2,1,0:T(8,128)(2,1)S(1)} %get-tuple-element.83.near, f32[256,128]{1,0:T(8,128)S(1)} %get-tuple-element.84.tok, f32[8,512]{1,0:T(8,128)S(1)} %get-tuple-element.85.goal, ...), custom_call_target="tpu_custom_call" | custom-call | tf_op jit(solution)/shard_map/cond/branch_1_fun/return_160_192/pallas_call | solution.py:518
  92.2 0.9 copy.23
Async XLA Ops:
  34.5 24.3 %copy-start = (bf16[256,1536]{1,0:T(8,128)(2,1)S(1)}, bf16[256,1536]{1,0:T(8,128)(2,1)}, u32[]{:S(2)}) copy-start(bf16[256,1536]{1,0:T(8,128)(2,1)} %hid_in.1) | copy-start | bytes 2359300

commit v2 on v0

--- a/solution.py
+++ b/solution.py
@@ -432,14 +432,17 @@
         halves[q] = pltpu.make_async_remote_copy(src_ref=ret.at[q + 1, pl.ds(0, cap)], dst_ref=half.at[q // 2], send_sem=half_send.at[q // 2], recv_sem=half_recv.at[q // 2], device_id=dev(flip(me, 1)), device_id_type=MESH)
         halves[q].start()
 
+    row = iota((chip_cap, cap), 0).astype(F32)
     for q in REMOTE:
-        row = iota((chip_cap, cap), 0).astype(F32)
         mine = (row == goal[q:q + 1, 0:cap]).astype(F32).astype(BF16)
+        for c in range(0, width, 512):
+            pack[q // 2 - 1, :, c:c + 512] = jnp.dot(mine, ret[q, 0:cap, c:c + 512], preferred_element_type=F32).astype(BF16)
+    for q in REMOTE:
         theirs = (row == goal[q:q + 1, lanes:lanes + cap]).astype(F32).astype(BF16)
         halves[q].wait_recv()
         for c in range(0, width, 512):
-            part = jnp.dot(mine, ret[q, 0:cap, c:c + 512], preferred_element_type=F32)
-            part = part + jnp.dot(theirs, half[q // 2, :, c:c + 512], preferred_element_type=F32)
+            part = jnp.dot(theirs, half[q // 2, :, c:c + 512], preferred_element_type=F32)
+            part = part + pack[q // 2 - 1, :, c:c + 512].astype(F32)
             pack[q // 2 - 1, :, c:c + 512] = part.astype(BF16)
         copies[q] = pltpu.make_async_remote_copy(src_ref=pack.at[q // 2 - 1], dst_ref=got.at[q // 2 - 1], send_sem=send.at[q // 2 - 1], recv_sem=recv.at[q // 2 - 1], device_id=dev(flip(me, q)), device_id_type=MESH)
         copies[q].start()

time: 95 us -> 94 us (0.989)
  Pallas kernels: 92.1 us -> 90.3 us
    pallas_call x1, Pallas kernels: 37.5 us -> 35.7 us  [return_call(): pl.pallas_call(functools.partial(return_kernel, cap, chip_cap), name=f're...]
where the time goes in v2:
time: 94 us; the launch traced here: 92.6 us
  Pallas kernels  90.3 us (96%)
    pallas_call x1, Pallas kernels, return_call(): pl.pallas_call(functools.partial(return_kernel, cap, chip_cap), name=f're...  35.7 us
    pallas_call x1, Pallas kernels, gather_call(): pl.pallas_call(functools.partial(gather_kernel, caps), name='gather_token...  33.9 us
    pallas_call x1, Pallas kernels, expert_call(): pl.pallas_call(functools.partial(expert_kernel, caps), name='experts', ou...  20.8 us

profile of v2, /device:TPU:0, one launch (start us, length us, event | category | flops | bytes accessed | tf_op | source)
XLA Modules:
  0.0 92.6 jit_solution(12822900182079207561)
XLA Ops:
  0.0 33.9 %gather_tokens.1 = (bf16[4,2,64,1536]{3,2,1,0:T(8,128)(2,1)S(1)}, bf16[4,6,64,1536]{3,2,1,0:T(8,128)(2,1)S(1)}, bf16[2,2,64,1536]{3,2,1,0:T(8,128)(2,1)S(1)}, f3...) custom-call(bf16[256,1536]{1,0:T(8,128)(2,1)} %hid_in.1, ...), custom_call_target="tpu_custom_call" | custom-call | tf_op jit(solution)/shard_map/gather_tokens/pallas_call | solution.py:271
  34.5 0.0 copy-start
  34.5 20.8 %experts.1 = (bf16[8,256,1536]{2,1,0:T(8,128)(2,1)S(1)}, bf16[4,1536,768]{2,1,0:T(8,128)(2,1)S(1)}, bf16[4,1536,768]{2,1,0:T(8,128)(2,1)S(1)}, bf16[4,768,1536]{2,1,0:T(8,128)(2,1)S(1)}) custom-call(s32[8,128]{1,0:T(8,128)S(1)} %get-tuple-element.118.info, ...), custom_call_target="tpu_custom_call", output_to_operand_aliasing={{1}: (3, {}), {2}: (4, {}), {3}: (5, {})} | custom-call | flops 21743271936 | bytes 84934656 | tf_op jit(solution)/shard_map/experts/pallas_call | solution.py:390
  55.2 0.0 copy-done
  55.2 36.4 %conditional.1 = (bf16[256,1536]{1,0:T(8,128)(2,1)S(1)}) conditional(s32[]{:T(128)} %bitcast.2, (bf16[8,256,1536]{2,1,0:T(8,128)(2,1)S(1)}, bf16[4,2,64,1536]{3,2,1,0:T(8,128)(2,1)S(1)}, f32[256,128]{1,0:T(8,128)S(1)}, f32[8,512]{1,0:T(8,128)S(1)}, bf16[256,1536]{1,0:T(8,128)(2,1)S(1)}, ...), branch_computations={%region_0.0_spmd, %region_1.0_spmd, %region_2.0_spmd, %region_3.0_... | conditional | bytes 8 | solution.py:566
  55.5 35.7 %return_160_192.1 = bf16[256,1536]{1,0:T(8,128)(2,1)S(1)} custom-call(bf16[8,256,1536]{2,1,0:T(8,128)(2,1)S(1)} %get-tuple-element.82.ret, bf16[4,2,64,1536]{3,2,1,0:T(8,128)(2,1)S(1)} %get-tuple-element.83.near, f32[256,128]{1,0:T(8,128)S(1)} %get-tuple-element.84.tok, f32[8,512]{1,0:T(8,128)S(1)} %get-tuple-element.85.goal, ...), custom_call_target="tpu_custom_call" | custom-call | tf_op jit(solution)/shard_map/cond/branch_1_fun/return_160_192/pallas_call | solution.py:521
  91.7 0.9 copy.23
Async XLA Ops:
  34.5 20.8 %copy-start = (bf16[256,1536]{1,0:T(8,128)(2,1)S(1)}, bf16[256,1536]{1,0:T(8,128)(2,1)}, u32[]{:S(2)}) copy-start(bf16[256,1536]{1,0:T(8,128)(2,1)} %hid_in.1) | copy-start | bytes 2359300
